TPU v7x, 32 devices: a whole 2x2x4 slice. The times are simulated.
32 devices in a mesh: fsdp: 4 (over y, x), dp: 8 (over z, core).
Axes of the slice: x: 2, y: 2, z: 4, core: 2. Of those that a mesh axis runs over, the one named last changes fastest.
Arguments:
- hidden_in: bfloat16 [8192, 1536], P(('fsdp', 'dp')), may hold values from -6 to 6
- lengths: int32 [32, 4], P(('fsdp', 'dp')), may hold values from 0 to 256, as said below
- norm_gain: bfloat16 [1536], P(('fsdp', 'dp')), may hold values from 0.5 to 1.5
- in_proj: bfloat16 [1536, 6448], P(('fsdp', 'dp')), may hold values from -0.15625 to 0.15625
- conv_weight: bfloat16 [3328, 4], P(('fsdp', 'dp')), may hold values from -3 to 3
- conv_bias: bfloat16 [3328], P(('fsdp', 'dp')), may hold values from -3 to 3
- gate_gain: bfloat16 [3072], P(('fsdp', 'dp')), may hold values from 0.5 to 1.5
- out_proj: bfloat16 [3072, 1536], P(('fsdp', 'dp')), may hold values from -0.109375 to 0.109375
- decay_log: float32 [48], replicated, may hold values from -3 to 1.5
- step_bias: float32 [48], replicated, may hold values from -5 to -2
- skip_gain: float32 [48], replicated, may hold values from 0.5 to 1.5
- grad_out: bfloat16 [8192, 1536], P(('fsdp', 'dp')), may hold values from -6 to 6
Outputs:
- hidden_out: bfloat16 [8192, 1536], P(('fsdp', 'dp'))
- grad_in: float32 [8192, 1536], P(('fsdp', 'dp'))
- grad_norm_gain: float32 [1536], P(('fsdp', 'dp'))
- grad_in_proj: float32 [1536, 6448], P(('fsdp', 'dp'))
- grad_conv_weight: float32 [3328, 4], P(('fsdp', 'dp'))
- grad_conv_bias: float32 [3328], P(('fsdp', 'dp'))
- grad_gate_gain: float32 [3072], P(('fsdp', 'dp'))
- grad_out_proj: float32 [3072, 1536], P(('fsdp', 'dp'))
- grad_decay_log: float32 [48], replicated
- grad_step_bias: float32 [48], replicated
- grad_skip_gain: float32 [48], replicated
Inputs may be any that keep to these rules, and one draw needn't show every extreme that they name: lengths[b] lists the sequences packed from the first row of block b on, in order; a length may be 0 (an empty slot); each block's lengths sum to at most 256 and the rows after that sum are padding; in every draw one block holds a single sequence of exactly 256 rows.
All inputs are finite; a program needn't handle non-finite values.
Results may differ from a plain program's by a relative error of at most 0.0063.
Values may be sent and summed in bfloat16 or wider, within the bound.
A program may use at most 192 MiB of HBM per device.

v0:
```python
import jax
import jax.numpy as jnp
from jax import lax
from jax.sharding import PartitionSpec as P

SPAN = 256
EPS = 1e-05
full_precision = lax.Precision.HIGHEST


def segment_ids(lens_row, row_count):
    ends = jnp.cumsum(lens_row)
    places = jnp.arange(row_count, dtype=jnp.int32)
    seg_ids = jnp.sum((places[:, None] >= ends[None, :]).astype(jnp.int32), axis=1)
    valid = (seg_ids < lens_row.shape[0]).astype(jnp.float32)
    return (seg_ids, valid)


def pre_norm(values, weight):
    return (
        values * lax.rsqrt(jnp.mean(values * values, axis=1, keepdims=True) + EPS) * weight[None, :]
    )


def convolve(inputs, weight, bias_row, seg_ids):
    kernel_len = weight.shape[1]
    summed = bias_row[None, :] + inputs * weight[:, kernel_len - 1][None, :]
    for offset in range(1, kernel_len):
        shifted = jnp.pad(inputs, ((offset, 0), (0, 0)))[:-offset]
        earlier = jnp.pad(seg_ids, (offset, 0), constant_values=-1)[:-offset]
        keep_mask = (earlier == seg_ids).astype(jnp.float32)
        summed = summed + shifted * keep_mask[:, None] * weight[:, kernel_len - 1 - offset][None, :]
    return summed


def state_scan(x_act, steps_dt, decay_rate, b_mat, c_mat, skips, seg_ids):
    row_count = x_act.shape[0]
    head_count = steps_dt.shape[1]
    head_dim = x_act.shape[1] // head_count
    state_dim = b_mat.shape[1]
    blocks = row_count // SPAN
    x_blocks = x_act.reshape(blocks, SPAN, head_count, head_dim)
    dt_blocks = steps_dt.reshape(blocks, SPAN, head_count)
    b_blocks = b_mat.reshape(blocks, SPAN, state_dim)
    c_blocks = c_mat.reshape(blocks, SPAN, state_dim)
    seg_blocks = seg_ids.reshape(blocks, SPAN)
    lower_tri = jnp.arange(SPAN)[:, None] >= jnp.arange(SPAN)[None, :]

    def block_step(scan_carry, block_in):
        old_state, prev_seg = scan_carry
        x_blk, dt_blk, b_blk, c_blk, seg_blk = block_in
        log_decay = jnp.cumsum(dt_blk * decay_rate[None, :], axis=0)
        same_seq = (seg_blk[:, None] == seg_blk[None, :]) & lower_tri
        spread = log_decay.T[:, :, None] - log_decay.T[:, None, :]
        decays = jnp.exp(jnp.where(same_seq[None], spread, -jnp.inf))
        inner_cb = jnp.dot(c_blk, b_blk.T, precision=full_precision)
        mixing = decays * inner_cb[None] * dt_blk.T[:, None, :]
        result = jnp.einsum("hts,shp->thp", mixing, x_blk, precision=full_precision)
        enters = (seg_blk == prev_seg).astype(jnp.float32)
        carried = jnp.einsum("tn,hpn->thp", c_blk, old_state, precision=full_precision)
        result = result + jnp.exp(log_decay)[:, :, None] * enters[:, None, None] * carried
        result = result + skips[None, :, None] * x_blk
        last_seg = seg_blk[-1]
        tail_wts = (
            jnp.exp(log_decay[-1][None, :] - log_decay)
            * (seg_blk == last_seg).astype(jnp.float32)[:, None]
            * dt_blk
        )
        new_state = jnp.einsum("sh,shp,sn->hpn", tail_wts, x_blk, b_blk, precision=full_precision)
        keep_old = jnp.exp(log_decay[-1]) * (prev_seg == last_seg).astype(jnp.float32)
        new_state = new_state + keep_old[:, None, None] * old_state
        return ((new_state, last_seg), result)

    start_state = (
        jnp.zeros((head_count, head_dim, state_dim), jnp.float32),
        jnp.array(-1, jnp.int32),
    )
    _, outputs = lax.scan(
        jax.checkpoint(block_step),
        start_state,
        (x_blocks, dt_blocks, b_blocks, c_blocks, seg_blocks),
    )
    return outputs.reshape(row_count, head_count * head_dim)


def mixer_branch(projected, kernel, shift_bias, gate, rates, biases, skips, seg_ids, valid):
    inner_dim = gate.shape[0]
    conv_dim = shift_bias.shape[0]
    state_dim = (conv_dim - inner_dim) // 2
    gate_in = projected[:, :inner_dim]
    conv_in = projected[:, inner_dim : inner_dim + conv_dim]
    dt_raw = projected[:, inner_dim + conv_dim :]
    activ = jax.nn.silu(convolve(conv_in, kernel, shift_bias, seg_ids))
    x_act = activ[:, :inner_dim]
    b_mat = activ[:, inner_dim : inner_dim + state_dim]
    c_mat = activ[:, inner_dim + state_dim :]
    steps_dt = jax.nn.softplus(dt_raw + biases[None, :])
    decay_rate = -jnp.exp(rates)
    scanned = state_scan(x_act, steps_dt, decay_rate, b_mat, c_mat, skips, seg_ids)
    gated = scanned * jax.nn.silu(gate_in)
    scale = lax.rsqrt(jnp.mean(gated * gated, axis=1, keepdims=True) + EPS)
    return gated * scale * gate[None, :] * valid[:, None]


def right_product(left, right):
    return lax.dot_general(
        left, right, (((1,), (1,)), ((), ())), preferred_element_type=jnp.float32
    )


def left_product(left, right):
    return lax.dot_general(
        left, right, (((0,), (0,)), ((), ())), preferred_element_type=jnp.float32
    )


def local(
    hidden_in,
    lengths,
    norm_gain,
    in_proj,
    conv_weight,
    conv_bias,
    gate_gain,
    out_proj,
    decay_log,
    step_bias,
    skip_gain,
    grad_out,
):
    row_count = hidden_in.shape[0]
    gain_all, kernel_all, shift_all, gate_all, out_all = (
        lax.all_gather(norm_gain, ("fsdp", "dp"), axis=0, tiled=True),
        lax.all_gather(conv_weight, ("fsdp", "dp"), axis=0, tiled=True),
        lax.all_gather(conv_bias, ("fsdp", "dp"), axis=0, tiled=True),
        lax.all_gather(gate_gain, ("fsdp", "dp"), axis=0, tiled=True),
        lax.all_gather(out_proj, ("fsdp", "dp"), axis=0, tiled=True),
    )
    seg_ids, valid = segment_ids(lengths[0], row_count)
    x_float = hidden_in.astype(jnp.float32)
    normed32, norm_back = jax.vjp(pre_norm, x_float, gain_all.astype(jnp.float32))
    normed = normed32.astype(jnp.bfloat16)
    columns = normed
    projected = jnp.dot(
        columns,
        lax.all_gather(in_proj, ("fsdp", "dp"), axis=0, tiled=True),
        preferred_element_type=jnp.float32,
    )

    def branch(proj_in, kernel, shift_bias, gate, rates, biases, skips):
        return mixer_branch(proj_in, kernel, shift_bias, gate, rates, biases, skips, seg_ids, valid)

    mixed32, branch_back = jax.vjp(
        branch,
        projected,
        kernel_all.astype(jnp.float32),
        shift_all.astype(jnp.float32),
        gate_all.astype(jnp.float32),
        decay_log,
        step_bias,
        skip_gain,
    )
    mixed = mixed32.astype(jnp.bfloat16)
    hidden_out = (x_float + jnp.dot(mixed, out_all, preferred_element_type=jnp.float32)).astype(
        jnp.bfloat16
    )
    columns = mixed
    grad_out_proj = lax.psum_scatter(
        left_product(columns, grad_out), ("fsdp", "dp"), scatter_dimension=0, tiled=True
    )
    grad_mixed = right_product(
        grad_out, lax.all_gather(out_proj, ("fsdp", "dp"), axis=0, tiled=True)
    )
    grad_proj, grad_kernel, grad_shift, grad_gate, grad_rates, grad_biases, grad_skips = (
        branch_back(grad_mixed)
    )
    proj_low = grad_proj.astype(jnp.bfloat16)
    columns = normed
    grad_in_proj = lax.psum_scatter(
        left_product(columns, proj_low), ("fsdp", "dp"), scatter_dimension=0, tiled=True
    )
    grad_normed = right_product(
        proj_low, lax.all_gather(in_proj, ("fsdp", "dp"), axis=0, tiled=True)
    )
    grad_x, grad_gain = norm_back(grad_normed)
    grad_in = grad_out.astype(jnp.float32) + grad_x
    small_sums = (
        lax.psum_scatter(grad_gain, ("fsdp", "dp"), scatter_dimension=0, tiled=True),
        lax.psum_scatter(grad_kernel, ("fsdp", "dp"), scatter_dimension=0, tiled=True),
        lax.psum_scatter(grad_shift, ("fsdp", "dp"), scatter_dimension=0, tiled=True),
        lax.psum_scatter(grad_gate, ("fsdp", "dp"), scatter_dimension=0, tiled=True),
    )
    head_sums = lax.psum((grad_rates, grad_biases, grad_skips), ("fsdp", "dp"))
    return (
        hidden_out,
        grad_in,
        small_sums[0],
        grad_in_proj,
        small_sums[1],
        small_sums[2],
        small_sums[3],
        grad_out_proj,
        head_sums[0],
        head_sums[1],
        head_sums[2],
    )


def solution(mesh):
    in_specs = (
        P(("fsdp", "dp"), None),
        P(("fsdp", "dp"), None),
        P(("fsdp", "dp")),
        P(("fsdp", "dp"), None),
        P(("fsdp", "dp"), None),
        P(("fsdp", "dp")),
        P(("fsdp", "dp")),
        P(("fsdp", "dp"), None),
        P(),
        P(),
        P(),
        P(("fsdp", "dp"), None),
    )
    out_specs = (
        P(("fsdp", "dp"), None),
        P(("fsdp", "dp"), None),
        P(("fsdp", "dp")),
        P(("fsdp", "dp"), None),
        P(("fsdp", "dp"), None),
        P(("fsdp", "dp")),
        P(("fsdp", "dp")),
        P(("fsdp", "dp"), None),
        P(),
        P(),
        P(),
    )
    return jax.shard_map(local, mesh=mesh, in_specs=in_specs, out_specs=out_specs, check_vma=False)
```

profile of v0, /device:TPU:0, one launch (start us, length us, event | category | flops | bytes accessed | tf_op | source)
XLA Modules:
  0.0 1067.1 jit_solution(12854662397712302054)
XLA Ops:
  11.3 44.1 %all-reduce.29 = (bf16[1536]{0:T(1024)(128)(2,1)S(1)}, bf16[3328]{0:T(1024)(128)(2,1)S(1)}, bf16[3072]{0:T(1024)(128)(2,1)S(1)}) all-reduce(bf16[1536]{0:T(1024)(128)(2,1)S(1)} %dynamic-update-slice.1, bf16[3328]{0:T(1024)(128)(2,1)S(1)} %dynamic-update-slice, ...), channel_id=1, replica_groups=mesh['fsdp'=4,'dp'=8] {'fsdp','dp'}, use_global_device_ids=true, to_apply=%add.22 | all-reduce | flops 7936 | bytes 31744
  56.6 41.5 %all-gather = bf16[32,104,4]{1,2,0:T(4,128)(2,1)S(1)} all-gather(bf16[1,104,4]{1,2,0:T(4,128)(2,1)} %bitcast.141), channel_id=1, replica_groups=mesh['fsdp'=4,'dp'=8] {'fsdp','dp'}, dimensions={0}, use_global_device_ids=true | all-gather | bytes 27456 | tf_op jit(solution)/shard_map/all_gather | solution.py:134
  100.5 1.4 fusion.56
  104.4 40.5 %all-gather.4.cloned.1.call-done = bf16[1536,6448]{1,0:T(8,128)(2,1)} async-done(((bf16[48,6448]{1,0:T(8,128)(2,1)}), bf16[1536,6448]{1,0:T(8,128)(2,1)}) %all-gather.4.cloned.1.call-update) | async-done | bytes 19808272 | tf_op jit(solution)/shard_map/all_gather | solution.py:146
  144.9 10.6 fusion.72
  155.8 2.5 copy-done.10
  159.2 1.8 copy.140
  161.0 1.9 reduce-window.30
  162.9 1.5 slice_reduce_fusion.2
  164.4 1.3 reduce-window.31
  167.7 4.8 fusion.32
  172.5 1.7 copy-done.11
  174.2 2.0 slice.112
  176.2 2.4 copy.138
  178.9 1.7 fusion.89
  180.6 3.5 fusion.67
  184.1 15.5 %fusion.38 = f32[256,48,64]{0,2,1:T(8,128)} fusion(f32[256,48,64]{0,2,1:T(8,128)S(1)} %bitcast.127, f32[256,48,64]{0,2,1:T(8,128)S(1)} %fusion.67, f32[48,256]{1,0:T(8,128)S(1)} %copy-done.30, f32[256,256]{1,0:T(8,128)S(1)} %fusion.89, f32[48,256]{1,0:T(8,128)S(1)} %copy_bitcast_fusion, pred[256,256]{1,0:T(8,128)(4,1)S(1)} %copy-done.23, ...), kind=kOutput, calls=%fused_computation.63 | convolution fusion | flops 2431647744 | bytes 9912512 | tf_op jit(solution)/shard_map/jvp()/while/body/eval_jaxpr/hts,shp->thp/dot_general | solution.py:58
  199.6 3.7 copy.144
  203.3 3.9 multiply_reduce_fusion.11
  209.7 18.0 %all-gather.6.cloned.1.call-done = bf16[3072,1536]{1,0:T(8,128)(2,1)} async-done(((bf16[96,1536]{1,0:T(8,128)(2,1)}), bf16[3072,1536]{1,0:T(8,128)(2,1)}) %all-gather.6.cloned.1.call-update) | async-done | bytes 9437200 | tf_op jit(solution)/shard_map/all_gather | solution.py:137
  227.7 6.6 multiply_reduce_fusion.8
  234.4 5.1 fusion.60
  239.5 3.5 copy.145
  247.1 2.7 multiply_reduce_fusion.9
  251.5 6.8 multiply_reduce_fusion.7
  258.3 18.9 %fusion.11 = (f32[48,256]{1,0:T(8,128)S(1)}, f32[48,256]{1,0:T(8,128)S(1)}, f32[48,256]{1,0:T(8,128)S(1)}, f32[256,256]{1,0:T(8,128)S(1)}) fusion(f32[48,256]{1,0:T(8,128)S(1)} %copy.152, f32[256,256]{1,0:T(8,128)S(1)} %fusion.101, f32[48,256]{1,0:T(8,128)S(1)} %copy.148, pred[256,256]{1,0:T(8,128)(4,1)S(1)} %compare_and_fusion, ...), kind=kOutput, calls=%fused_computation.14 | convolution fusion | flops 2456711168 | bytes 7127040 | tf_op jit(solution)/shard_map/transpose(jvp())/while/body/eval_jaxpr/checkpoint/hts,shp->thp/dot_general | solution.py:58
  278.7 2.5 reduce-window.43
  282.1 7.1 fusion.64
  289.3 13.4 %bitcast_add_fusion = f32[256,48,64]{0,2,1:T(8,128)} fusion(f32[256,48,64]{0,2,1:T(8,128)S(1)} %bitcast.126, f32[256,48,64]{0,2,1:T(8,128)} %get-tuple-element.199, f32[48,256]{1,0:T(8,128)S(1)} %copy.152, f32[256,256]{1,0:T(8,128)S(1)} %fusion.101, f32[48,256]{1,0:T(8,128)S(1)} %copy-done.29, pred[256,256]{1,0:T(8,128)(4,1)S(1)} %compare_and_fusion, ...), kind=kOutput, calls=%fused_computation.58 | convolution fusion | flops 2431647744 | bytes 9912512 | tf_op jit(solution)/shard_map/transpose(jvp())/while/body/eval_jaxpr/checkpoint/hts,shp->thp/dot_general | solution.py:58
  302.7 3.9 copy.159
  306.7 7.1 fusion.61
  314.8 7.1 fusion.95
  324.3 1.6 copy.156
  325.9 2.5 fusion.96
  329.5 1.9 multiply_multiply_fusion
  331.4 2.9 fusion.29
  335.0 13.5 %fusion.54 = (f32[1536]{0:T(1024)}, f32[256]{0:T(256)S(1)}, f32[256,1536]{1,0:T(8,128)}) fusion(bf16[256,1536]{1,0:T(8,128)(2,1)} %param.12, f32[256]{0:T(256)S(1)} %fusion.83, f32[1536]{0:T(1024)S(1)} %convert_element_type.81, bf16[1536,6448]{1,0:T(8,128)(2,1)} %all-gather.4.cloned.1.call-done, f32[256,3072]{1,0:T(8,128)} %get-tuple-element.179, ...), kind=kOutput, calls=%fused_computation.87 | convolution fusion | flops 5078616064 | bytes 28784640 | tf_op jit(solution)/shard_map/dot_general | solution.py:106
  348.6 9.1 fusion.94
  357.8 18.9 %fusion.70 = f32[1536,6448]{1,0:T(8,128)} fusion(bf16[256,1536]{1,0:T(8,128)(2,1)} %param.12, f32[1536]{0:T(1024)S(1)} %convert_element_type.81, f32[256]{0:T(256)S(1)} %fusion.83, f32[256,3072]{1,0:T(8,128)} %get-tuple-element.179, f32[256,3328]{1,0:T(8,128)} %fusion.29, f32[256,48]{1,0:T(8,128)S(1)} %copy-done.18), kind=kOutput, calls=%fused_computation.108 | convolution fusion | flops 5077438464 | bytes 47012864 | tf_op jit(solution)/shard_map/dot_general | solution.py:112
  377.4 3.5 fusion.55
  380.9 7.2 fusion.44
  388.1 84.8 %all-reduce.32.cloned.1.call-done = (f32[1536]{0:T(1024)}, f32[3328,4]{0,1:T(4,128)}, f32[3328]{0:T(1024)}, f32[3072]{0:T(1024)}, f32[48]{0:T(128)}, /*index=5*/f32[48]{0:T(128)}, f32[48]{0:T(128)}) async-done(((f32[1536]{0:T(1024)}, f32[3328,4]{0,1:T(4,128)}, f32[3328]{0:T(1024)}, f32[3072]{0:T(1024)}, f32[48]{0:T(128)}, /*index=5*/f32[48]{0:T(128)}, f32[48]{0:T(128)}), (f32[1536]{0:T(1024)}, ...) | async-done | bytes 85584
  472.9 1.3 dynamic-slice.11
  474.2 1.3 dynamic-slice.8
  475.5 1.3 dynamic-slice.10
  476.7 1.3 constant_dynamic-slice_fusion
  478.1 209.4 %reduce-scatter.6.cloned.1.call-done = f32[96,1536]{1,0:T(8,128)} async-done(((f32[3072,1536]{1,0:T(8,128)}), f32[96,1536]{1,0:T(8,128)}) %reduce-scatter.6.cloned.1.call-update) | async-done | bytes 589840 | tf_op jit(solution)/shard_map/reduce_scatter | solution.py:168
  687.5 369.6 %reduce-scatter.4.cloned.1.call-done = f32[48,6448]{1,0:T(8,128)} async-done(((f32[1536,6448]{1,0:T(8,128)}), f32[48,6448]{1,0:T(8,128)}) %reduce-scatter.4.cloned.1.call-update) | async-done | bytes 1238032 | tf_op jit(solution)/shard_map/reduce_scatter | solution.py:179
  (175 shorter events, 32.7 us)
Async XLA Ops:
  7.2 137.7 %all-gather.4.cloned.1.call-start = ((), (), s32[]{:S(2)}) async-start(), calls=%async_computation.2 | async-start | bytes 20680704 | tf_op jit(solution)/shard_map/all_gather | solution.py:146
  7.9 219.8 %all-gather.6.cloned.1.call-start = ((), (), s32[]{:S(2)}) async-start(), calls=%async_computation.3 | async-start | bytes 9732096 | tf_op jit(solution)/shard_map/all_gather | solution.py:137
  8.7 464.2 %all-reduce.32.cloned.1.call-start = ((), (), s32[]{:S(2)}) async-start(), calls=%async_computation.6 | async-start | bytes 183296
  155.6 2.8 copy-start.10
  155.6 2.8 copy-start.42
  155.6 2.8 copy-start.45
  158.4 14.1 %copy-start.3 = (f32[256,3328]{1,0:T(8,128)}, f32[256,3328]{1,0:T(8,128)S(1)}, u32[]{:S(2)}) copy-start(f32[256,3328]{1,0:T(8,128)S(1)} %slice.107) | copy-start | bytes 10223620
  176.2 2.4 copy-start.17
  176.2 2.4 copy-start.35
  176.2 2.5 copy-start.44
  178.6 21.0 %copy-start.8 = (f32[256,3072]{0,1:T(8,128)}, f32[256,3072]{0,1:T(8,128)S(1)}, u32[]{:S(2)}) copy-start(f32[256,3072]{0,1:T(8,128)S(1)} %copy.138) | copy-start | bytes 9437188
  178.6 5.5 copy-start.23
  178.6 5.4 copy-start.30
  178.7 5.4 copy-start.46
  207.2 27.2 %copy-start.5 = (f32[256,3072]{1,0:T(8,128)}, f32[256,3072]{1,0:T(8,128)S(1)}, u32[]{:S(2)}) copy-start(f32[256,3072]{1,0:T(8,128)S(1)} %get-tuple-element.173) | copy-start | bytes 9437188
  209.7 41.4 %copy-start.15 = (f32[256,128]{1,0:T(8,128)}, f32[256,128]{1,0:T(8,128)S(1)}, u32[]{:S(2)}) copy-start(f32[256,128]{1,0:T(8,128)S(1)} %get-tuple-element.113) | copy-start | bytes 393220
  227.7 6.6 copy-start.40
  227.7 6.6 copy-start.7
  227.7 6.7 copy-start.20
  227.7 6.7 copy-start.31
  239.5 5.4 copy-start.19
  244.9 33.5 %copy-start.34 = (f32[256]{0:T(256)}, f32[256]{0:T(256)S(1)}, u32[]{:S(2)}) copy-start(f32[256]{0:T(256)S(1)} %get-tuple-element.192) | copy-start | bytes 3076
  245.2 1.9 copy-start
  245.3 4.5 copy-start.43
  251.0 27.4 %copy-start.13 = (f32[48,2,128]{0,2,1:T(8,128)}, f32[48,2,128]{0,2,1:T(8,128)S(1)}, u32[]{:S(2)}) copy-start(f32[48,2,128]{0,2,1:T(8,128)S(1)} %copy.147) | copy-start | bytes 147460
  251.1 7.2 copy-start.28
  251.5 6.8 copy-start.1
  251.5 6.8 copy-start.9
  278.2 11.0 %copy-start.14 = (f32[256,48]{1,0:T(8,128)}, f32[256,48]{1,0:T(8,128)S(1)}, u32[]{:S(2)}) copy-start(f32[256,48]{1,0:T(8,128)S(1)} %copy.166) | copy-start | bytes 147460
  278.3 10.9 %copy-start.41 = (f32[48]{0:T(128)}, f32[48]{0:T(128)S(1)}, u32[]{:S(2)}) copy-start(f32[48]{0:T(128)S(1)} %get-tuple-element.190) | copy-start | bytes 580
  278.6 10.7 copy-start.29
  278.6 10.7 copy-start.47
  282.1 7.1 copy-start.2
  306.6 7.2 copy-start.16
  306.6 8.2 copy-start.33
  306.7 8.1 copy-start.4
  331.4 2.9 copy-start.24
  331.4 2.9 copy-start.25
  331.4 2.9 copy-start.26
  331.4 2.9 copy-start.27
  331.4 3.6 copy-start.18
  335.0 13.6 %copy-start.6 = (f32[256,3072]{1,0:T(8,128)S(1)}, f32[256,3072]{1,0:T(8,128)}, u32[]{:S(2)}) copy-start(f32[256,3072]{1,0:T(8,128)} %copy-done.5) | copy-start | bytes 9437188
  335.0 13.6 %copy-start.21 = (f32[3072]{0:T(1024)S(1)}, f32[3072]{0:T(1024)}, u32[]{:S(2)}) copy-start(f32[3072]{0:T(1024)} %convert_element_type.89) | copy-start | bytes 36868
  335.0 13.6 %copy-start.32 = (f32[256]{0:T(256)S(1)}, f32[256]{0:T(256)}, u32[]{:S(2)}) copy-start(f32[256]{0:T(256)} %fusion.84) | copy-start | bytes 3076
  335.0 13.6 %copy-start.36 = (f32[256]{0:T(256)S(1)}, f32[256]{0:T(256)}, u32[]{:S(2)}) copy-start(f32[256]{0:T(256)} %get-tuple-element.193) | copy-start | bytes 3076
  348.5 338.9 %reduce-scatter.6.cloned.1.call-start = ((), (), s32[]{:S(2)}) async-start(), calls=%async_computation.5 | async-start | bytes 19464192 | tf_op jit(solution)/shard_map/reduce_scatter | solution.py:168
  357.8 699.2 %reduce-scatter.4.cloned.1.call-start = ((), (), s32[]{:S(2)}) async-start(), calls=%async_computation.4 | async-start | bytes 41361408 | tf_op jit(solution)/shard_map/reduce_scatter | solution.py:179
  376.8 4.1 copy-start.12
  (5 other events, 6.0 us)
Sparse Core Ops, SparseCore 0:
  11.0 133.8 all-gather.3
  147.9 79.7 all-gather.5
  348.7 124.1 all-reduce.31
  479.7 207.6 reduce-scatter.5
  694.3 362.6 reduce-scatter.3
where the time goes:
time: 1070 us
  waiting for transfers between devices  724 us (68%)
  matrix products  144 us (13%)
  blocking collectives  85.6 us (8%)
  other arithmetic  50.8 us (5%)
  local copies, waits for them, and re-layouts  47.5 us (4%)
  between operations  15.4 us (1%)
    reduce_scatter x1, waiting for transfers between devices, local(): lax.psum_scatter(left_product(columns, proj_low), ('fsdp', 'dp'), scatter...  370 us
    reduce_scatter x1, waiting for transfers between devices, local(): lax.psum_scatter(left_product(columns, grad_out), ('fsdp', 'dp'), scatter...  209 us
    unnamed x6, waiting for transfers between devices  86.2 us
    dot_general x3, matrix products, block_step(): result = jnp.einsum('hts,shp->thp', mixing, x_blk, precision=full_precision)  47.8 us
    unnamed x1, blocking collectives  44.1 us
    all_gather x1, blocking collectives, local(): lax.all_gather(conv_weight, ('fsdp', 'dp'), axis=0, tiled=True)  41.5 us
    all_gather x1, waiting for transfers between devices, local(): lax.all_gather(in_proj, ('fsdp', 'dp'), axis=0, tiled=True)  40.5 us
    dot_general x2, matrix products, left_product(): lax.dot_general(left, right, (((0,), (0,)), ((), ())), preferred_element_...  28.1 us
  transfers between devices with their start and end apart: 5, of which 5 were waited for; matrix products, arithmetic and copies ran while one was open for 11% of the time, Pallas kernels for 0%

commit v1 on v0

--- a/solution.py
+++ b/solution.py
@@ -6,6 +6,15 @@
 SPAN = 256
 EPS = 1e-05
 full_precision = lax.Precision.HIGHEST
+
+
+def report_paths(array_in):
+    buffers = []
+    for _ in range(lax.axis_size(("fsdp", "dp"))):
+        buffers.append(array_in)
+    e_now = jnp.stack(buffers)
+    v_next = lax.all_to_all(e_now, axis_name=("fsdp", "dp"), split_axis=0, concat_axis=0)
+    return jnp.concatenate(v_next, axis=0)
 
 
 def segment_ids(lens_row, row_count):
@@ -141,11 +150,7 @@
     normed32, norm_back = jax.vjp(pre_norm, x_float, gain_all.astype(jnp.float32))
     normed = normed32.astype(jnp.bfloat16)
     columns = normed
-    projected = jnp.dot(
-        columns,
-        lax.all_gather(in_proj, ("fsdp", "dp"), axis=0, tiled=True),
-        preferred_element_type=jnp.float32,
-    )
+    projected = jnp.dot(columns, report_paths(in_proj), preferred_element_type=jnp.float32)
 
     def branch(proj_in, kernel, shift_bias, gate, rates, biases, skips):
         return mixer_branch(proj_in, kernel, shift_bias, gate, rates, biases, skips, seg_ids, valid)

time: 1070 us -> 1580 us (1.48)
  blocking collectives: 85.6 us -> 637 us
  waiting for transfers between devices: 724 us -> 667 us
    all_gather x1, blocking collectives: 41.5 us -> 599 us  [local(): lax.all_gather(conv_weight, ('fsdp', 'dp'), axis=0, tiled=True)]
    all_gather x1, waiting for transfers between devices: 40.5 us -> 0.01 us  [local(): lax.all_gather(in_proj, ('fsdp', 'dp'), axis=0, tiled=True)]
    all_gather x1, waiting for transfers between devices: 18 us -> 0.02 us  [local(): lax.all_gather(out_proj, ('fsdp', 'dp'), axis=0, tiled=True)]
  transfers between devices with their start and end apart: 5 -> 6, of which waited for: 5 -> 3; matrix products, arithmetic and copies ran while one was open for 11% -> 13% of each run, Pallas kernels for 0% -> 0%
where the time goes in v1:
time: 1580 us; the launch traced here: 1570 us
  waiting for transfers between devices  667 us (42%)
  blocking collectives  637 us (40%)
  matrix products  149 us (9%)
  local copies, waits for them, and re-layouts  46.6 us (3%)
  other arithmetic  42.8 us (3%)
  between operations  15.8 us (1%)
    all_gather x1, blocking collectives, local(): lax.all_gather(conv_weight, ('fsdp', 'dp'), axis=0, tiled=True)  599 us
    reduce_scatter x1, waiting for transfers between devices, local(): lax.psum_scatter(left_product(columns, proj_low), ('fsdp', 'dp'), scatter...  370 us
    reduce_scatter x1, waiting for transfers between devices, local(): lax.psum_scatter(left_product(columns, grad_out), ('fsdp', 'dp'), scatter...  209 us
    unnamed x6, waiting for transfers between devices  88.2 us
    dot_general x3, matrix products, block_step(): result = jnp.einsum('hts,shp->thp', mixing, x_blk, precision=full_precision)  52.5 us
    unnamed x1, blocking collectives  37.6 us
  transfers between devices with their start and end apart: 6, of which 3 were waited for; matrix products, arithmetic and copies ran while one was open for 13% of the time, Pallas kernels for 0%

profile of v1, /device:TPU:0, one launch (start us, length us, event | category | flops | bytes accessed | tf_op | source)
XLA Modules:
  0.0 1565.8 jit_solution(16890562832798359960)
XLA Ops:
  7.2 7.8 stack.2
  15.1 7.4 all-to-all-start
  24.1 599.4 %all-gather = bf16[32,104,4]{1,2,0:T(4,128)(2,1)S(1)} all-gather(bf16[1,104,4]{1,2,0:T(4,128)(2,1)S(1)} %bitcast.142), channel_id=1, replica_groups=mesh['fsdp'=4,'dp'=8] {'fsdp','dp'}, dimensions={0}, use_global_device_ids=true | all-gather | bytes 27456 | tf_op jit(solution)/shard_map/all_gather | solution.py:143
  624.4 37.6 %all-reduce.29 = (bf16[1536]{0:T(1024)(128)(2,1)S(1)}, bf16[3328]{0:T(1024)(128)(2,1)S(1)}, bf16[3072]{0:T(1024)(128)(2,1)S(1)}) all-reduce(bf16[1536]{0:T(1024)(128)(2,1)S(1)} %dynamic-update-slice.1, bf16[3328]{0:T(1024)(128)(2,1)S(1)} %dynamic-update-slice, ...), channel_id=1, replica_groups=mesh['fsdp'=4,'dp'=8] {'fsdp','dp'}, use_global_device_ids=true, to_apply=%add.22 | all-reduce | flops 7936 | bytes 31744
  665.8 9.8 fusion.72
  675.9 2.6 copy-done.8
  678.5 4.0 fusion.32
  682.5 1.7 copy-done.9
  684.2 2.0 slice.112
  686.2 2.4 copy.138
  688.6 1.1 broadcast_multiply_fusion.1
  691.5 1.3 fusion.89
  692.9 3.5 fusion.67
  696.4 16.6 %fusion.38 = f32[256,48,64]{0,2,1:T(8,128)} fusion(f32[256,48,64]{0,2,1:T(8,128)S(1)} %bitcast.128, f32[256,48,64]{0,2,1:T(8,128)S(1)} %fusion.67, f32[48,256]{1,0:T(8,128)S(1)} %copy-done.32, f32[256,256]{1,0:T(8,128)S(1)} %fusion.89, f32[48,256]{1,0:T(8,128)S(1)} %copy_bitcast_fusion, pred[256,256]{1,0:T(8,128)(4,1)} %compare_and_fusion.1, f32[48]{0:T(128)} %param.22, ...), kind=kOutput, calls=%fused_computation.63 | convolution fusion | flops 2431647744 | bytes 9912512 | tf_op jit(solution)/shard_map/jvp()/while/body/eval_jaxpr/hts,shp->thp/dot_general | solution.py:67
  713.1 3.5 copy.144
  716.6 3.9 multiply_reduce_fusion.11
  720.6 7.5 multiply_reduce_fusion.8
  728.1 5.1 fusion.60
  733.2 2.4 copy.145
  735.6 2.0 fusion.100
  739.6 1.3 reduce-window.34
  745.0 1.3 fusion.101
  746.3 21.7 %fusion.11 = (f32[48,256]{1,0:T(8,128)}, f32[48,256]{1,0:T(8,128)}, f32[48,256]{1,0:T(8,128)}, f32[256,256]{1,0:T(8,128)}) fusion(f32[48,256]{1,0:T(8,128)} %copy.152, f32[256,256]{1,0:T(8,128)S(1)} %fusion.101, f32[48,256]{1,0:T(8,128)} %copy.148, pred[256,256]{1,0:T(8,128)(4,1)S(1)} %compare_and_fusion, f32[256,48,64]{0,2,1:T(8,128)} %bitcast.129, ...), kind=kOutput, calls=%fused_computation.14 | convolution fusion | flops 2456711168 | bytes 7127040 | tf_op jit(solution)/shard_map/transpose(jvp())/while/body/eval_jaxpr/checkpoint/hts,shp->thp/dot_general | solution.py:67
  770.0 4.2 multiply_reduce_fusion.9
  775.1 6.6 multiply_reduce_fusion.7
  783.4 14.1 bitcast_add_fusion
  797.5 3.5 copy.159
  801.1 2.7 reduce-window.43
  804.3 7.1 fusion.64
  812.0 5.1 fusion.61
  817.6 6.6 fusion.95
  824.3 1.5 fusion.96
  827.0 1.2 multiply_multiply_fusion
  828.2 2.9 fusion.29
  831.1 13.3 fusion.54
  844.6 9.1 fusion.94
  853.8 19.2 %fusion.70 = f32[1536,6448]{1,0:T(8,128)} fusion(bf16[256,1536]{1,0:T(8,128)(2,1)} %param.12, f32[1536]{0:T(1024)S(1)} %convert_element_type.81, f32[256]{0:T(256)S(1)} %fusion.83, f32[256,3072]{1,0:T(8,128)} %get-tuple-element.179, f32[256,3328]{1,0:T(8,128)} %fusion.29, f32[256,48]{1,0:T(8,128)S(1)} %get-tuple-element.170), kind=kOutput, calls=%fused_computation.108 | convolution fusion | flops 5077438464 | bytes 47012864 | tf_op jit(solution)/shard_map/dot_general | solution.py:121
  873.6 3.5 fusion.55
  877.1 7.2 fusion.44
  884.4 86.8 %all-reduce.32.cloned.1.call-done = (f32[1536]{0:T(1024)}, f32[3328,4]{0,1:T(4,128)}, f32[3328]{0:T(1024)}, f32[3072]{0:T(1024)}, f32[48]{0:T(128)}, /*index=5*/f32[48]{0:T(128)}, f32[48]{0:T(128)}) async-done(((f32[1536]{0:T(1024)}, f32[3328,4]{0,1:T(4,128)}, f32[3328]{0:T(1024)}, f32[3072]{0:T(1024)}, f32[48]{0:T(128)}, /*index=5*/f32[48]{0:T(128)}, f32[48]{0:T(128)}), (f32[1536]{0:T(1024)}, ...) | async-done | bytes 85584
  971.2 1.3 dynamic-slice.8
  972.5 1.3 dynamic-slice.10
  973.7 1.3 dynamic-slice.11
  975.0 1.3 constant_dynamic-slice_fusion
  976.3 209.4 %reduce-scatter.6.cloned.1.call-done = f32[96,1536]{1,0:T(8,128)} async-done(((f32[3072,1536]{1,0:T(8,128)}), f32[96,1536]{1,0:T(8,128)}) %reduce-scatter.6.cloned.1.call-update) | async-done | bytes 589840 | tf_op jit(solution)/shard_map/reduce_scatter | solution.py:173
  1185.7 369.6 %reduce-scatter.4.cloned.1.call-done = f32[48,6448]{1,0:T(8,128)} async-done(((f32[1536,6448]{1,0:T(8,128)}), f32[48,6448]{1,0:T(8,128)}) %reduce-scatter.4.cloned.1.call-update) | async-done | bytes 1238032 | tf_op jit(solution)/shard_map/reduce_scatter | solution.py:184
  1555.3 1.2 copy.184
  1556.5 1.2 copy.185
  (196 shorter events, 22.8 us)
Async XLA Ops:
  15.0 9.1 copy-start.49
  15.0 608.6 %copy-start.50 = (bf16[48]{0:T(256)(128)(2,1)S(1)}, bf16[48]{0:T(256)(128)(2,1)}, u32[]{:S(2)}) copy-start(bf16[48]{0:T(256)(128)(2,1)} %param.14) | copy-start | bytes 292
  15.0 608.8 %copy-start.51 = (bf16[104]{0:T(256)(128)(2,1)S(1)}, bf16[104]{0:T(256)(128)(2,1)}, u32[]{:S(2)}) copy-start(bf16[104]{0:T(256)(128)(2,1)} %param.17) | copy-start | bytes 628
  15.0 609.1 %copy-start.52 = (bf16[96]{0:T(256)(128)(2,1)S(1)}, bf16[96]{0:T(256)(128)(2,1)}, u32[]{:S(2)}) copy-start(bf16[96]{0:T(256)(128)(2,1)} %param.18) | copy-start | bytes 580
  15.0 647.5 %copy-start.53 = (s32[1,4]{1,0:T(1,128)S(1)}, s32[1,4]{1,0:T(1,128)}, u32[]{:S(2)}) copy-start(s32[1,4]{1,0:T(1,128)} %param.13) | copy-start | bytes 52
  15.1 648.5 %copy-start.11 = (bf16[256,1536]{1,0:T(8,128)(2,1)S(1)}, bf16[256,1536]{1,0:T(8,128)(2,1)}, u32[]{:S(2)}) copy-start(bf16[256,1536]{1,0:T(8,128)(2,1)} %param.12) | copy-start | bytes 2359300
  15.1 648.8 %copy-start.55 = (f32[48]{0:T(128)S(1)}, f32[48]{0:T(128)}, u32[]{:S(2)}) copy-start(f32[48]{0:T(128)} %param.20) | copy-start | bytes 580
  15.1 650.7 %all-to-all-start = ((bf16[32,48,6448]{2,1,0:T(8,128)(2,1)}), bf16[32,48,6448]{2,1,0:T(8,128)(2,1)}, u32[]{:S(2)}, u32[]{:S(2)}) async-start(bf16[32,48,6448]{2,1,0:T(8,128)(2,1)} %stack.2), calls=%async_computation | async-start | bytes 40108032 | tf_op jit(solution)/shard_map/all_to_all | solution.py:16
  22.5 698.0 %all-gather.4.cloned.1.call-start = ((), (), s32[]{:S(2)}) async-start(), calls=%async_computation.3 | async-start | bytes 9732096 | tf_op jit(solution)/shard_map/all_gather | solution.py:146
  23.3 807.8 %all-gather.6.cloned.1.call-start = ((), (), s32[]{:S(2)}) async-start(), calls=%async_computation.4 | async-start | bytes 20680704 | tf_op jit(solution)/shard_map/all_gather | solution.py:188
  24.0 947.2 %all-reduce.32.cloned.1.call-start = ((), (), s32[]{:S(2)}) async-start(), calls=%async_computation.7 | async-start | bytes 183296
  663.6 14.8 copy-start.19
  663.6 14.8 copy-start.21
  663.6 14.8 copy-start.23
  663.6 14.8 copy-start.25
  664.5 24.1 %copy-start.45 = (f32[48]{0:T(128)}, f32[48]{0:T(128)S(1)}, u32[]{:S(2)}) copy-start(f32[48]{0:T(128)S(1)} %exponential_negate_fusion) | copy-start | bytes 580
  665.0 13.4 copy-start.35
  665.1 13.4 copy-start.37
  665.1 13.4 copy-start.39
  688.6 24.4 %copy-start.7 = (f32[256,3072]{0,1:T(8,128)}, f32[256,3072]{0,1:T(8,128)S(1)}, u32[]{:S(2)}) copy-start(f32[256,3072]{0,1:T(8,128)S(1)} %copy.138) | copy-start | bytes 9437188
  691.4 5.1 copy-start.32
  720.5 7.6 copy-start.4
  720.5 7.6 copy-start.33
  720.5 7.5 copy-start.6
  735.6 32.5 %copy-start = (f32[256,3072]{0,1:T(8,128)}, f32[256,3072]{0,1:T(8,128)S(1)}, u32[]{:S(2)}) copy-start(f32[256,3072]{0,1:T(8,128)S(1)} %copy.145) | copy-start | bytes 9437188
  745.0 23.1 %copy-start.27 = (pred[256,256]{1,0:T(8,128)(4,1)}, pred[256,256]{1,0:T(8,128)(4,1)S(1)}, u32[]{:S(2)}) copy-start(pred[256,256]{1,0:T(8,128)(4,1)S(1)} %compare_and_fusion) | copy-start | bytes 196612
  746.3 21.7 %copy-start.15 = (f32[256,256]{1,0:T(8,128)}, f32[256,256]{1,0:T(8,128)S(1)}, u32[]{:S(2)}) copy-start(f32[256,256]{1,0:T(8,128)S(1)} %fusion.101) | copy-start | bytes 786436
  797.5 6.7 copy-start.29
  801.0 10.4 copy-start.13
  801.0 10.4 copy-start.14
  804.2 7.8 copy-start.1
  804.3 13.2 copy-start.10
  811.4 6.2 copy-start.3
  811.4 6.2 copy-start.36
  811.4 6.2 copy-start.38
  811.4 6.2 copy-start.40
  817.5 6.7 copy-start.46
  817.6 6.7 copy-start.48
  817.6 8.2 copy-start.56
  817.6 9.4 copy-start.22
  817.6 9.4 copy-start.24
  817.6 9.4 copy-start.26
  831.1 13.4 copy-start.5
  831.1 13.4 copy-start.18
  831.1 13.5 copy-start.34
  831.1 13.5 copy-start.42
  844.5 341.3 %reduce-scatter.6.cloned.1.call-start = ((), (), s32[]{:S(2)}) async-start(), calls=%async_computation.6 | async-start | bytes 19464192 | tf_op jit(solution)/shard_map/reduce_scatter | solution.py:173
  853.7 701.6 %reduce-scatter.4.cloned.1.call-start = ((), (), s32[]{:S(2)}) async-start(), calls=%async_computation.5 | async-start | bytes 41361408 | tf_op jit(solution)/shard_map/reduce_scatter | solution.py:184
  (15 other events, 33.7 us)
Sparse Core Ops, SparseCore 0:
  26.4 181.5 all-gather.3
  211.0 297.4 all-gather.5
  844.6 126.5 all-reduce.31
  978.0 207.6 reduce-scatter.5
  1192.6 362.6 reduce-scatter.3
